TPU v7x, 256 devices: a whole 4x4x8 slice. The times are simulated.
256 devices in a mesh: gx: 16 (over z, core), gy: 4 (over x), gz: 4 (over y).
Axes of the slice: x: 4, y: 4, z: 8, core: 2. Of those that a mesh axis runs over, the one named last changes fastest.
Arguments:
- velocity: float32 [3, 1024, 128, 512], P(None, 'gx', 'gz', 'gy'), may hold values from -6 to 6
- tile_turbine: int32 [16, 4, 4, 2], P('gx', 'gz', 'gy'), may hold values from 0 to 63
- tile_plane: int32 [16, 4, 4, 2], P('gx', 'gz', 'gy'), may hold values from 0 to 63
- tile_weight: bfloat16 [16, 4, 4, 2, 384, 4096], P('gx', 'gz', 'gy'), may hold values from -0.09375 to 0.09375
- chord: float32 [64, 384], replicated, may hold values from 0.25 to 1
Outputs:
- predicted: float32 [3, 1024, 128, 512], P(None, 'gx', 'gz', 'gy')
- forces: float32 [64, 1152], replicated
All inputs are finite; a program needn't handle non-finite values.
Results may differ from a plain program's by a relative error of at most 0.0032.
Values sent between devices are 32-bit elements; how exact they have to be, the bound alone decides.
No kernel may reach another device: no remote copies, remote signals or barrier semaphores. Data moves between devices by JAX's collectives and lax.ppermute only.
A program may use at most 128 MiB of HBM per device.

v0:
```python
import jax
import jax.numpy as jnp
from jax import lax
from jax.sharding import PartitionSpec as P

DIRS = (-3, -1, -2)


def padded_2(block, sides, width):
    for axis, dim in sides:
        count = lax.axis_size(axis)
        forward = [(i, i + 1) for i in range(count - 1)]
        backward = [(target, source) for source, target in forward]
        low = lax.ppermute(
            lax.slice_in_dim(block, block.shape[dim] - width, None, axis=dim), axis, forward
        )
        high = lax.ppermute(lax.slice_in_dim(block, 0, width, axis=dim), axis, backward)
        block = jnp.concatenate([low, block, high], axis=dim)
    return block


def shifted(p, axis, step):
    idx = [slice(1, -1), slice(1, -1), slice(1, -1)]
    idx[axis + 3] = slice(1 + step, p.shape[axis] - 1 + step)
    lead = [slice(None)] * (p.ndim - 3)
    return p[tuple(lead + idx)]


def strain_viscosity(p):
    grads = [
        [0.5 * (shifted(p[c], DIRS[d], 1) - shifted(p[c], DIRS[d], -1)) for d in range(3)]
        for c in range(3)
    ]
    total = jnp.zeros_like(grads[0][0])
    for c in range(3):
        for d in range(3):
            strain = 0.5 * (grads[c][d] + grads[d][c])
            total = total + strain * strain
    return 0.05 + 1.0 * jnp.sqrt(2.0 * total + 1e-06)


def advance(padded, nu_padded):
    nu_here = shifted(nu_padded, -1, 0)
    result = []
    for c in range(3):
        center = shifted(padded[c], -1, 0)
        advect = jnp.zeros_like(center)
        spread = jnp.zeros_like(center)
        for d in range(3):
            upper = shifted(padded[c], DIRS[d], 1)
            lower = shifted(padded[c], DIRS[d], -1)
            advect = advect + shifted(padded[d], -1, 0) * 0.5 * (upper - lower)
            nu_up = 0.5 * (nu_here + shifted(nu_padded, DIRS[d], 1))
            nu_low = 0.5 * (nu_here + shifted(nu_padded, DIRS[d], -1))
            spread = spread + nu_up * (upper - center) - nu_low * (center - lower)
        result.append(center + 0.25 * (spread - advect))
    return jnp.stack(result)


def actuate(velocity_probe, coef):
    rows = velocity_probe.shape[0]
    parts = velocity_probe.reshape(rows, 3, -1)
    magnitude = jnp.sqrt(jnp.sum(parts * parts, axis=1) + 1e-06)
    return (-2.0 * coef[:, None, :] * magnitude[:, None, :] * parts).reshape(rows, -1)


def body(velocity, tile_turbine, tile_plane, tile_weight, chord):
    cx = velocity.shape[1]
    vertical_coord = velocity.shape[2]
    spanwise_coord = velocity.shape[3]
    tile_count = tile_turbine.shape[3]
    actuator_count = tile_weight.shape[4]
    nturb = chord.shape[0]
    turbine_list = tile_turbine.reshape(tile_count)
    rotor_planes = tile_plane.reshape(tile_count)
    spread_weights = tile_weight.reshape(
        tile_count, actuator_count, vertical_coord * spanwise_coord
    )
    flat = velocity.reshape(3, cx, vertical_coord * spanwise_coord)
    picks = (rotor_planes[:, None] == jnp.arange(cx, dtype=jnp.int32)[None, :]).astype(jnp.float32)
    tiles = jnp.einsum("sx,cxq->scq", picks, flat, precision=lax.Precision.HIGHEST).astype(
        jnp.bfloat16
    )
    block_local = jnp.einsum(
        "spq,scq->scp", spread_weights, tiles, preferred_element_type=jnp.float32
    )
    owning_block = (turbine_list[:, None] == jnp.arange(nturb, dtype=jnp.int32)[None, :]).astype(
        jnp.float32
    )
    partial_sample = jnp.einsum(
        "yr,yw->rw",
        owning_block,
        block_local.reshape(tile_count, -1),
        precision=lax.Precision.HIGHEST,
    )
    sample = lax.psum(partial_sample, ("gx", "gy", "gz"))
    forces = actuate(sample, chord)
    tile_force = jnp.dot(owning_block, forces, precision=lax.Precision.HIGHEST).astype(jnp.bfloat16)
    forces_sent = jnp.einsum(
        "axz,ahx->ahz",
        spread_weights,
        tile_force.reshape(tile_count, 3, actuator_count),
        preferred_element_type=jnp.float32,
    )
    impulse = jnp.einsum(
        "sx,scq->cxq", picks, forces_sent, precision=lax.Precision.HIGHEST
    ).reshape(3, cx, vertical_coord, spanwise_coord)
    padded = padded_2(velocity, (("gx", 1), ("gy", 3), ("gz", 2)), 1)
    viscosity = strain_viscosity(padded)
    nu_padded = padded_2(viscosity, (("gx", 0), ("gy", 2), ("gz", 1)), 1)
    predicted = advance(padded, nu_padded) + impulse
    return (predicted, forces)


def solution(mesh):
    placed = (
        P(None, "gx", "gz", "gy"),
        P("gx", "gz", "gy", None),
        P("gx", "gz", "gy", None),
        P("gx", "gz", "gy", None, None, None),
        P(),
    )
    return jax.shard_map(
        body,
        mesh=mesh,
        in_specs=placed,
        out_specs=(P(None, "gx", "gz", "gy"), P()),
        check_vma=False,
    )
```

profile of v0, /device:TPU:32, one launch (start us, length us, event | category | flops | bytes accessed | tf_op | source)
XLA Modules:
  0.0 375.6 jit_solution(18153228875391277242)
XLA Ops:
  8.0 1.9 collective-permute-start
  10.0 3.6 collective-permute-start.1
  13.6 2.9 reshape.28
  17.7 4.7 %fusion.4 = f32[1,2,3,384]{3,2,1,0:T(4,128)S(1)} fusion(bf16[1,1,1,2,384,4096]{5,4,3,2,1,0:T(8,128)(2,1)} %param.8, bf16[2,3,4096]{2,0,1:T(2,128)(2,1)S(1)} %convolution_convert_fusion), kind=kOutput, calls=%fused_computation.11 | convolution fusion | flops 18874368 | bytes 6349824 | tf_op jit(solution)/shard_map/spq,scq->scp/dot_general | solution.py:84
  22.7 3.9 %fusion.29 = (f32[3,66,32,1]{3,2,1,0:T(8,128)}, f32[3,66,32,1]{3,2,1,0:T(8,128)}) fusion(f32[3,66,32,128]{3,2,1,0:T(8,128)S(1)} %constant_dynamic-update-slice_fusion), kind=kLoop, calls=%fused_computation.83 | loop fusion | bytes 101376 | tf_op jit(solution)/shard_map/slice | solution.py:15
  26.6 2.8 copy.27
  29.4 3.4 collective-permute-start.2
  32.8 2.8 copy.28
  38.1 2.7 copy.29
  41.6 2.7 copy.30
  44.3 4.0 %pad_maximum_fusion.22 = (f32[3,66,1,130]{3,2,1,0:T(1,128)}, f32[3,66,1,130]{3,2,1,0:T(1,128)}) fusion(f32[3,66,32,1]{3,2,1,0:T(8,128)} %copy.30, f32[3,66,32,128]{3,2,1,0:T(8,128)S(1)} %constant_dynamic-update-slice_fusion, f32[3,66,32,1]{3,2,1,0:T(8,128)} %copy.29), kind=kLoop, calls=%fused_computation.61 | loop fusion | flops 102960 | bytes 3500640 | tf_op jit(solution)/shard_map/slice | solution.py:15
  48.3 4.2 %collective-permute-start.4 = (f32[3,66,1,130]{3,2,1,0:T(1,128)}, f32[3,66,1,130]{3,2,1,0:T(1,128)}, u32[]{:S(2)}, u32[]{:S(2)}) collective-permute-start(f32[3,66,1,130]{3,2,1,0:T(1,128)} %get-tuple-element.6), channel_id=1, source_target_pairs={{0,1},{1,2},{2,3},{4,5},{5,6},{6,7},{8,9},{9,10},{10,11},{12,13},{... | collective-permute-start | bytes 308888 | tf_op jit(solution)/shard_map/ppermute | solution.py:14
  53.9 235.0 %all-reduce.2.cloned.1.call-done = f32[64,1152]{1,0:T(8,128)} async-done(((f32[64,1152]{1,0:T(8,128)}), f32[64,1152]{1,0:T(8,128)}) %all-reduce.2.cloned.1.call-update) | async-done | bytes 294928 | tf_op jit(solution)/shard_map/psum | solution.py:96
  288.9 1.9 mul.296
  292.6 1.9 reduce_sum.9
  295.7 6.0 %pad_maximum_fusion = f32[3,66,34,130]{3,2,1,0:T(8,128)S(1)} fusion(f32[3,66,1,130]{3,2,1,0:T(1,128)} %collective-permute-done.5, f32[3,66,32,1]{3,2,1,0:T(8,128)} %copy.30, f32[3,66,32,128]{3,2,1,0:T(8,128)S(1)} %constant_dynamic-update-slice_fusion, f32[3,66,32,1]{3,2,1,0:T(8,128)} %copy.29, f32[3,66,1,130]{3,2,1,0:T(1,128)} %collective-permute-done.4), kind=kLoop, calls=%fused_computation | loop fusion | flops 3500640 | bytes 7001280 | tf_op jit(solution)/shard_map/concatenate | solution.py:18
  302.2 4.8 %sqrt_add_fusion = f32[64,32,128]{2,1,0:T(8,128)S(1)} fusion(f32[66,34,130]{2,1,0:T(8,128)S(1)} %get-tuple-element.10, f32[66,34,130]{2,1,0:T(8,128)S(1)} %get-tuple-element.8, f32[66,34,130]{2,1,0:T(8,128)S(1)} %get-tuple-element.9), kind=kLoop, calls=%fused_computation.46 | loop fusion | flops 9961472 | bytes 19922944 | tf_op jit(solution)/shard_map/add | solution.py:39
  308.1 3.5 collective-permute-start.6
  311.6 1.9 collective-permute-start.7
  313.8 2.8 collective-permute-done.7
  319.7 1.9 copy.31
  322.9 1.9 copy.33
  324.7 4.5 %collective-permute-start.9 = (f32[66,32,1]{0,1,2:T(8,128)S(1)}, f32[66,32,1]{0,1,2:T(8,128)S(1)}, u32[]{:S(2)}, u32[]{:S(2)}) collective-permute-start(f32[66,32,1]{0,1,2:T(8,128)S(1)} %copy.33), channel_id=1, source_target_pairs={{0,4},{4,8},{8,12},{1,5},{5,9},{9,13},{2,6},{6,10},{10,14},{3,7},{... | collective-permute-start | bytes 25352 | tf_op jit(solution)/shard_map/ppermute | solution.py:14
  329.3 3.7 fusion
  333.0 1.9 copy.32
  334.9 1.9 copy.34
  336.8 1.9 pad_maximum_fusion.23
  339.9 4.8 %collective-permute-start.11 = (f32[66,1,130]{2,1,0:T(1,128)S(1)}, f32[66,1,130]{2,1,0:T(1,128)S(1)}, u32[]{:S(2)}, u32[]{:S(2)}) collective-permute-start(f32[66,1,130]{2,1,0:T(1,128)S(1)} %get-tuple-element.11), channel_id=1, source_target_pairs={{0,1},{1,2},{2,3},{4,5},{5,6},{6,7},{8,9},{9,10},{10,11},{12,13},{... | collective-permute-start | bytes 102968 | tf_op jit(solution)/shard_map/ppermute | solution.py:14
  348.9 5.8 %add_bitcast_fusion.2 = f32[1,64,32,128]{3,2,1,0:T(8,128)S(1)} fusion(f32[66,34,130]{2,1,0:T(8,128)S(1)} %copy-done.3, f32[66,34,130]{2,1,0:T(8,128)S(1)} %get-tuple-element.8, f32[66,34,130]{2,1,0:T(8,128)S(1)} %copy-done.1, f32[64,32,128]{2,1,0:T(8,128)S(1)} %copy-done.5, f32[1,32,128]{2,1,0:T(8,128)S(1)} %collective-permute-done.6, ...), kind=kLoop, calls=%fused_computation.45 | loop fusion | flops 15990784 | bytes 11652640 | tf_op jit(solution)/shard_map/stack | solution.py:57
  354.7 5.8 %add_bitcast_fusion.1 = f32[1,64,32,128]{3,2,1,0:T(8,128)S(1)} fusion(f32[66,34,130]{2,1,0:T(8,128)S(1)} %get-tuple-element.8, f32[66,34,130]{2,1,0:T(8,128)S(1)} %copy-done.3, f32[66,34,130]{2,1,0:T(8,128)S(1)} %copy-done.1, f32[64,32,128]{2,1,0:T(8,128)S(1)} %copy-done.5, f32[1,32,128]{2,1,0:T(8,128)S(1)} %collective-permute-done.6, ...), kind=kLoop, calls=%fused_computation.44 | loop fusion | flops 15990784 | bytes 11652640 | tf_op jit(solution)/shard_map/stack | solution.py:57
  360.5 5.8 %add_bitcast_fusion = f32[1,64,32,128]{3,2,1,0:T(8,128)S(1)} fusion(f32[66,34,130]{2,1,0:T(8,128)S(1)} %copy-done.1, f32[66,34,130]{2,1,0:T(8,128)S(1)} %copy-done.3, f32[66,34,130]{2,1,0:T(8,128)S(1)} %get-tuple-element.8, f32[64,32,128]{2,1,0:T(8,128)S(1)} %copy-done.5, f32[1,32,128]{2,1,0:T(8,128)S(1)} %collective-permute-done.6, ...), kind=kLoop, calls=%fused_computation.43 | loop fusion | flops 15990784 | bytes 11652640 | tf_op jit(solution)/shard_map/stack | solution.py:57
  366.4 2.4 bitcast_add_fusion
  (63 shorter events, 21.5 us)
Async XLA Ops:
  7.2 281.8 %all-reduce.2.cloned.1.call-start = ((), (), s32[]{:S(2)}) async-start(), calls=%async_computation | async-start | bytes 589824 | tf_op jit(solution)/shard_map/psum | solution.py:96
  8.0 14.3 %collective-permute-start = (f32[3,1,32,128]{3,2,1,0:T(8,128)S(1)}, f32[3,1,32,128]{3,2,1,0:T(8,128)S(1)}, u32[]{:S(2)}, u32[]{:S(2)}) collective-permute-start(f32[3,1,32,128]{3,2,1,0:T(8,128)S(1)} %get-tuple-element.16), channel_id=1, source_target_pairs={{0,16},{16,32},{32,48},{48,64},{64,80},{80,96},{96,112},{112,128},... | collective-permute-start | bytes 147464 | tf_op jit(solution)/shard_map/ppermute | solution.py:14
  10.0 6.6 %copy-start.12 = (s32[1,1,1,2]{3,2,1,0:T(1,128)S(1)}, s32[1,1,1,2]{3,2,1,0:T(1,128)}, u32[]{:S(2)}) copy-start(s32[1,1,1,2]{3,2,1,0:T(1,128)} %param.7) | copy-start | bytes 28
  10.0 12.7 %collective-permute-start.1 = (f32[3,1,32,128]{3,2,1,0:T(8,128)S(1)}, f32[3,1,32,128]{3,2,1,0:T(8,128)S(1)}, u32[]{:S(2)}, u32[]{:S(2)}) collective-permute-start(f32[3,1,32,128]{3,2,1,0:T(8,128)S(1)} %get-tuple-element.15), channel_id=1, source_target_pairs={{16,0},{32,16},{48,32},{64,48},{80,64},{96,80},{112,96},{128,112},... | collective-permute-start | bytes 147464 | tf_op jit(solution)/shard_map/ppermute | solution.py:17
  17.6 4.7 %copy-start.8 = (f32[3,64,32,128]{3,2,1,0:T(8,128)S(1)}, f32[3,64,32,128]{3,2,1,0:T(8,128)}, u32[]{:S(2)}) copy-start(f32[3,64,32,128]{3,2,1,0:T(8,128)} %param.5) | copy-start | bytes 9437188
  26.6 10.3 %copy-start.11 = (s32[1,1,1,2]{3,2,1,0:T(1,128)S(1)}, s32[1,1,1,2]{3,2,1,0:T(1,128)}, u32[]{:S(2)}) copy-start(s32[1,1,1,2]{3,2,1,0:T(1,128)} %param.6) | copy-start | bytes 28
  29.4 8.7 %collective-permute-start.2 = (f32[3,66,32,1]{1,2,3,0:T(8,128)S(1)}, f32[3,66,32,1]{1,2,3,0:T(8,128)S(1)}, u32[]{:S(2)}, u32[]{:S(2)}) collective-permute-start(f32[3,66,32,1]{1,2,3,0:T(8,128)S(1)} %copy.27), channel_id=1, source_target_pairs={{0,4},{4,8},{8,12},{1,5},{5,9},{9,13},{2,6},{6,10},{10,14},{3,7},{... | collective-permute-start | bytes 76040 | tf_op jit(solution)/shard_map/ppermute | solution.py:14
  35.6 6.0 %collective-permute-start.3 = (f32[3,66,32,1]{1,2,3,0:T(8,128)S(1)}, f32[3,66,32,1]{1,2,3,0:T(8,128)S(1)}, u32[]{:S(2)}, u32[]{:S(2)}) collective-permute-start(f32[3,66,32,1]{1,2,3,0:T(8,128)S(1)} %copy.28), channel_id=1, source_target_pairs={{4,0},{8,4},{12,8},{5,1},{9,5},{13,9},{6,2},{10,6},{14,10},{7,3},{... | collective-permute-start | bytes 76040 | tf_op jit(solution)/shard_map/ppermute | solution.py:17
  48.3 247.4 %collective-permute-start.4 = (f32[3,66,1,130]{3,2,1,0:T(1,128)}, f32[3,66,1,130]{3,2,1,0:T(1,128)}, u32[]{:S(2)}, u32[]{:S(2)}) collective-permute-start(f32[3,66,1,130]{3,2,1,0:T(1,128)} %get-tuple-element.6), channel_id=1, source_target_pairs={{0,1},{1,2},{2,3},{4,5},{5,6},{6,7},{8,9},{9,10},{10,11},{12,13},{... | collective-permute-start | bytes 308888 | tf_op jit(solution)/shard_map/ppermute | solution.py:14
  52.4 243.2 %collective-permute-start.5 = (f32[3,66,1,130]{3,2,1,0:T(1,128)}, f32[3,66,1,130]{3,2,1,0:T(1,128)}, u32[]{:S(2)}, u32[]{:S(2)}) collective-permute-start(f32[3,66,1,130]{3,2,1,0:T(1,128)} %get-tuple-element.7), channel_id=1, source_target_pairs={{1,0},{2,1},{3,2},{5,4},{6,5},{7,6},{9,8},{10,9},{11,10},{13,12},{... | collective-permute-start | bytes 308888 | tf_op jit(solution)/shard_map/ppermute | solution.py:17
  288.9 6.6 %copy-start.9 = (f32[64,1152]{1,0:T(8,128)S(1)}, f32[64,1152]{1,0:T(8,128)}, u32[]{:S(2)}) copy-start(f32[64,1152]{1,0:T(8,128)} %all-reduce.2.cloned.1.call-done) | copy-start | bytes 884740
  295.6 17.9 %copy-start.10 = (f32[64,1152]{1,0:T(8,128)}, f32[64,1152]{1,0:T(8,128)S(1)}, u32[]{:S(2)}) copy-start(f32[64,1152]{1,0:T(8,128)S(1)} %mul.301) | copy-start | bytes 884740
  302.2 4.8 %copy-start = (f32[66,34,130]{2,1,0:T(8,128)}, f32[66,34,130]{2,1,0:T(8,128)S(1)}, u32[]{:S(2)}) copy-start(f32[66,34,130]{2,1,0:T(8,128)S(1)} %get-tuple-element.9) | copy-start | bytes 3500644
  302.2 4.8 %copy-start.2 = (f32[66,34,130]{2,1,0:T(8,128)}, f32[66,34,130]{2,1,0:T(8,128)S(1)}, u32[]{:S(2)}) copy-start(f32[66,34,130]{2,1,0:T(8,128)S(1)} %get-tuple-element.10) | copy-start | bytes 3500644
  307.1 1.0 copy-start.4
  308.1 5.8 %collective-permute-start.6 = (f32[1,32,128]{2,1,0:T(8,128)S(1)}, f32[1,32,128]{2,1,0:T(8,128)S(1)}, u32[]{:S(2)}, u32[]{:S(2)}) collective-permute-start(f32[1,32,128]{2,1,0:T(8,128)S(1)} %get-tuple-element.20), channel_id=1, source_target_pairs={{16,0},{32,16},{48,32},{64,48},{80,64},{96,80},{112,96},{128,112},... | collective-permute-start | bytes 49160 | tf_op jit(solution)/shard_map/ppermute | solution.py:17
  311.6 5.1 %collective-permute-start.7 = (f32[1,32,128]{2,1,0:T(8,128)S(1)}, f32[1,32,128]{2,1,0:T(8,128)S(1)}, u32[]{:S(2)}, u32[]{:S(2)}) collective-permute-start(f32[1,32,128]{2,1,0:T(8,128)S(1)} %get-tuple-element.19), channel_id=1, source_target_pairs={{0,16},{16,32},{32,48},{48,64},{64,80},{80,96},{96,112},{112,128},... | collective-permute-start | bytes 49160 | tf_op jit(solution)/shard_map/ppermute | solution.py:14
  321.6 11.4 %collective-permute-start.8 = (f32[66,32,1]{0,1,2:T(8,128)S(1)}, f32[66,32,1]{0,1,2:T(8,128)S(1)}, u32[]{:S(2)}, u32[]{:S(2)}) collective-permute-start(f32[66,32,1]{0,1,2:T(8,128)S(1)} %copy.31), channel_id=1, source_target_pairs={{4,0},{8,4},{12,8},{5,1},{9,5},{13,9},{6,2},{10,6},{14,10},{7,3},{... | collective-permute-start | bytes 25352 | tf_op jit(solution)/shard_map/ppermute | solution.py:17
  324.7 10.2 %collective-permute-start.9 = (f32[66,32,1]{0,1,2:T(8,128)S(1)}, f32[66,32,1]{0,1,2:T(8,128)S(1)}, u32[]{:S(2)}, u32[]{:S(2)}) collective-permute-start(f32[66,32,1]{0,1,2:T(8,128)S(1)} %copy.33), channel_id=1, source_target_pairs={{0,4},{4,8},{8,12},{1,5},{5,9},{9,13},{2,6},{6,10},{10,14},{3,7},{... | collective-permute-start | bytes 25352 | tf_op jit(solution)/shard_map/ppermute | solution.py:14
  338.6 8.2 %collective-permute-start.10 = (f32[66,1,130]{2,1,0:T(1,128)S(1)}, f32[66,1,130]{2,1,0:T(1,128)S(1)}, u32[]{:S(2)}, u32[]{:S(2)}) collective-permute-start(f32[66,1,130]{2,1,0:T(1,128)S(1)} %get-tuple-element.12), channel_id=1, source_target_pairs={{1,0},{2,1},{3,2},{5,4},{6,5},{7,6},{9,8},{10,9},{11,10},{13,12},{... | collective-permute-start | bytes 102968 | tf_op jit(solution)/shard_map/ppermute | solution.py:17
  339.9 6.9 %collective-permute-start.11 = (f32[66,1,130]{2,1,0:T(1,128)S(1)}, f32[66,1,130]{2,1,0:T(1,128)S(1)}, u32[]{:S(2)}, u32[]{:S(2)}) collective-permute-start(f32[66,1,130]{2,1,0:T(1,128)S(1)} %get-tuple-element.11), channel_id=1, source_target_pairs={{0,1},{1,2},{2,3},{4,5},{5,6},{6,7},{8,9},{9,10},{10,11},{12,13},{... | collective-permute-start | bytes 102968 | tf_op jit(solution)/shard_map/ppermute | solution.py:14
  344.7 2.2 copy-start.5
  344.7 2.2 copy-start.6
  344.7 2.2 copy-start.7
  346.3 1.8 copy-start.1
  346.3 2.6 copy-start.3
Sparse Core Ops, SparseCore 0:
  38.2 250.7 all-reduce.1
where the time goes:
time: 376 us
  waiting for transfers between devices  239 us (64%)
  other arithmetic  42.5 us (11%)
  local copies, waits for them, and re-layouts  34.3 us (9%)
  starting transfers between devices  33.2 us (9%)
  between operations  14.5 us (4%)
  matrix products  12.4 us (3%)
    psum x1, waiting for transfers between devices, body(): sample = lax.psum(partial_sample, ('gx', 'gy', 'gz'))  235 us
    ppermute x6, starting transfers between devices, padded_2(): lax.ppermute(lax.slice_in_dim(block, block.shape[dim] - width, None, axis...  20.7 us
    another operation x3, other arithmetic, advance(): return jnp.stack(result)  17.4 us
    ppermute x6, starting transfers between devices, padded_2(): lax.ppermute(lax.slice_in_dim(block, 0, width, axis=dim), axis, backward)  12.5 us
    slice x5, local copies, waits for them, and re-layouts, padded_2(): lax.slice_in_dim(block, block.shape[dim] - width, None, axis=dim)  10.3 us
    concatenate x3, other arithmetic, padded_2(): block = jnp.concatenate([low, block, high], axis=dim)  9.16 us
  transfers between devices with their start and end apart: 13, of which 3 were waited for; matrix products, arithmetic and copies ran while one was open for 10% of the time, Pallas kernels for 0%

commit v1 on v0

--- a/solution.py
+++ b/solution.py
@@ -93,7 +93,7 @@
         block_local.reshape(tile_count, -1),
         precision=lax.Precision.HIGHEST,
     )
-    sample = lax.psum(partial_sample, ("gx", "gy", "gz"))
+    sample = jnp.sum(lax.all_gather(partial_sample, ("gx", "gy", "gz")), axis=0)
     forces = actuate(sample, chord)
     tile_force = jnp.dot(owning_block, forces, precision=lax.Precision.HIGHEST).astype(jnp.bfloat16)
     forces_sent = jnp.einsum(

time: 376 us -> 294 us (0.78); the launches traced: 376 us -> 290 us
  waiting for transfers between devices: 239 us -> 128 us
  other arithmetic: 42.5 us -> 67.9 us
    psum x1 -> x0, waiting for transfers between devices: 235 us -> none  [body(): sample = lax.psum(partial_sample, ('gx', 'gy', 'gz'))]
    all_gather x0 -> x1, waiting for transfers between devices: none -> 108 us  [body(): sample = jnp.sum(lax.all_gather(partial_sample, ('gx', 'gy', 'gz')), axis=0)]
    reduce_sum x0 -> x1, other arithmetic: none -> 23.7 us  [body(): sample = jnp.sum(lax.all_gather(partial_sample, ('gx', 'gy', 'gz')), axis=0)]
    ppermute x6, waiting for transfers between devices: 0.81 us -> 15.5 us  [padded_2(): lax.ppermute(lax.slice_in_dim(block, 0, width, axis=dim), axis, backward)]
    another operation x3, other arithmetic: 17.4 us -> 26.6 us  [advance(): return jnp.stack(result)]
  transfers between devices with their start and end apart: 13 -> 13, of which waited for: 3 -> 8; matrix products, arithmetic and copies ran while one was open for 10% -> 24% of each run, Pallas kernels for 0% -> 0%
where the time goes in v1:
time: 294 us; the launch traced here: 290 us
  waiting for transfers between devices  128 us (44%)
  other arithmetic  67.9 us (23%)
  local copies, waits for them, and re-layouts  34.8 us (12%)
  starting transfers between devices  30.9 us (11%)
  between operations  14.5 us (5%)
  matrix products  14.1 us (5%)
    all_gather x1, waiting for transfers between devices, body(): sample = jnp.sum(lax.all_gather(partial_sample, ('gx', 'gy', 'gz')), axis=0)  108 us
    another operation x3, other arithmetic, advance(): return jnp.stack(result)  26.6 us
    reduce_sum x1, other arithmetic, body(): sample = jnp.sum(lax.all_gather(partial_sample, ('gx', 'gy', 'gz')), axis=0)  23.7 us
    ppermute x6, starting transfers between devices, padded_2(): lax.ppermute(lax.slice_in_dim(block, block.shape[dim] - width, None, axis...  17.8 us
    ppermute x6, waiting for transfers between devices, padded_2(): lax.ppermute(lax.slice_in_dim(block, 0, width, axis=dim), axis, backward)  15.5 us
    ppermute x6, starting transfers between devices, padded_2(): lax.ppermute(lax.slice_in_dim(block, 0, width, axis=dim), axis, backward)  13.1 us
    slice x5, local copies, waits for them, and re-layouts, padded_2(): lax.slice_in_dim(block, block.shape[dim] - width, None, axis=dim)  10.5 us
    concatenate x3, other arithmetic, padded_2(): block = jnp.concatenate([low, block, high], axis=dim)  6.08 us
  transfers between devices with their start and end apart: 13, of which 8 were waited for; matrix products, arithmetic and copies ran while one was open for 24% of the time, Pallas kernels for 0%

profile of v1, /device:TPU:32, one launch (start us, length us, event | category | flops | bytes accessed | tf_op | source)
XLA Modules:
  0.0 289.8 jit_solution(5761058461444359643)
XLA Ops:
  7.2 4.6 %reshape.28 = f32[3,64,4096]{2,1,0:T(8,128)} reshape(f32[3,64,32,128]{3,2,1,0:T(8,128)} %param.5) | data formatting | bytes 6291456 | tf_op jit(solution)/shard_map/reshape | solution.py:79
  11.8 3.0 %convolution_convert_fusion = bf16[2,3,4096]{2,0,1:T(2,128)(2,1)S(1)} fusion(f32[3,64,4096]{2,1,0:T(8,128)} %reshape.28, s32[2]{0:T(128)S(1)} %bitcast.52), kind=kOutput, calls=%fused_computation.5 | convolution fusion | flops 18899072 | bytes 3194888 | tf_op jit(solution)/shard_map/sx,cxq->scq/dot_general | solution.py:81
  14.8 4.5 %fusion.4 = f32[1,2,3,384]{3,2,1,0:T(4,128)S(1)} fusion(bf16[1,1,1,2,384,4096]{5,4,3,2,1,0:T(8,128)(2,1)} %param.8, bf16[2,3,4096]{2,0,1:T(2,128)(2,1)S(1)} %convolution_convert_fusion), kind=kOutput, calls=%fused_computation.11 | convolution fusion | flops 18874368 | bytes 6349824 | tf_op jit(solution)/shard_map/spq,scq->scp/dot_general | solution.py:84
  23.3 3.6 %collective-permute-start.1 = (f32[3,1,32,128]{3,2,1,0:T(8,128)S(1)}, f32[3,1,32,128]{3,2,1,0:T(8,128)S(1)}, u32[]{:S(2)}, u32[]{:S(2)}) collective-permute-start(f32[3,1,32,128]{3,2,1,0:T(8,128)S(1)} %get-tuple-element.15), channel_id=1, source_target_pairs={{16,0},{32,16},{48,32},{64,48},{80,64},{96,80},{112,96},{128,112},... | collective-permute-start | bytes 147464 | tf_op jit(solution)/shard_map/ppermute | solution.py:17
  26.9 2.2 constant_dynamic-update-slice_fusion.1
  29.2 3.9 %fusion.29 = (f32[3,66,32,1]{3,2,1,0:T(8,128)}, f32[3,66,32,1]{3,2,1,0:T(8,128)}) fusion(f32[3,66,32,128]{3,2,1,0:T(8,128)S(1)} %constant_dynamic-update-slice_fusion), kind=kLoop, calls=%fused_computation.83 | loop fusion | bytes 101376 | tf_op jit(solution)/shard_map/slice | solution.py:15
  33.1 2.8 copy.27
  35.9 3.4 %collective-permute-start.2 = (f32[3,66,32,1]{1,2,3,0:T(8,128)S(1)}, f32[3,66,32,1]{1,2,3,0:T(8,128)S(1)}, u32[]{:S(2)}, u32[]{:S(2)}) collective-permute-start(f32[3,66,32,1]{1,2,3,0:T(8,128)S(1)} %copy.27), channel_id=1, source_target_pairs={{0,4},{4,8},{8,12},{1,5},{5,9},{9,13},{2,6},{6,10},{10,14},{3,7},{... | collective-permute-start | bytes 76040 | tf_op jit(solution)/shard_map/ppermute | solution.py:14
  39.3 2.8 copy.28
  43.4 2.7 copy.29
  46.1 2.2 collective-permute-done.3
  48.3 2.7 copy.30
  50.9 3.9 %pad_maximum_fusion.22 = (f32[3,66,1,130]{3,2,1,0:T(1,128)S(1)}, f32[3,66,1,130]{3,2,1,0:T(1,128)S(1)}) fusion(f32[3,66,32,1]{3,2,1,0:T(8,128)} %copy.30, f32[3,66,32,128]{3,2,1,0:T(8,128)} %copy-done.4, f32[3,66,32,1]{3,2,1,0:T(8,128)} %copy.29), kind=kLoop, calls=%fused_computation.61 | loop fusion | flops 102960 | bytes 3500640 | tf_op jit(solution)/shard_map/slice | solution.py:15
  54.8 3.8 %collective-permute-start.4 = (f32[3,66,1,130]{3,2,1,0:T(1,128)S(1)}, f32[3,66,1,130]{3,2,1,0:T(1,128)S(1)}, u32[]{:S(2)}, u32[]{:S(2)}) collective-permute-start(f32[3,66,1,130]{3,2,1,0:T(1,128)S(1)} %get-tuple-element.6), channel_id=1, source_target_pairs={{0,1},{1,2},{2,3},{4,5},{5,6},{6,7},{8,9},{9,10},{10,11},{12,13},{... | collective-permute-start | bytes 308888 | tf_op jit(solution)/shard_map/ppermute | solution.py:14
  60.1 3.6 %collective-permute-done.4 = f32[3,66,1,130]{3,2,1,0:T(1,128)S(1)} collective-permute-done((f32[3,66,1,130]{3,2,1,0:T(1,128)S(1)}, f32[3,66,1,130]{3,2,1,0:T(1,128)S(1)}, u32[]{:S(2)}, u32[]{:S(2)}) %collective-permute-start.4) | collective-permute-done | bytes 102992 | tf_op jit(solution)/shard_map/ppermute | solution.py:14
  63.7 4.1 %collective-permute-done.5 = f32[3,66,1,130]{3,2,1,0:T(1,128)S(1)} collective-permute-done((f32[3,66,1,130]{3,2,1,0:T(1,128)S(1)}, f32[3,66,1,130]{3,2,1,0:T(1,128)S(1)}, u32[]{:S(2)}, u32[]{:S(2)}) %collective-permute-start.5) | collective-permute-done | bytes 102992 | tf_op jit(solution)/shard_map/ppermute | solution.py:17
  67.9 4.0 %pad_maximum_fusion = f32[3,66,34,130]{3,2,1,0:T(8,128)S(1)} fusion(f32[3,66,1,130]{3,2,1,0:T(1,128)S(1)} %collective-permute-done.5, f32[3,66,32,1]{3,2,1,0:T(8,128)S(1)} %copy-done.9, f32[3,66,32,128]{3,2,1,0:T(8,128)S(1)} %copy-done.5, f32[3,66,32,1]{3,2,1,0:T(8,128)S(1)} %copy-done.8, f32[3,66,1,130]{3,2,1,0:T(1,128)S(1)} %collective-permute-done.4), kind=kLoop, calls=%fused_computation | loop fusion | flops 3500640 | bytes 7001280 | tf_op jit(solution)/shard_map/concatenate | solution.py:18
  72.4 4.8 %sqrt_add_fusion = f32[64,32,128]{2,1,0:T(8,128)S(1)} fusion(f32[66,34,130]{2,1,0:T(8,128)S(1)} %get-tuple-element.10, f32[66,34,130]{2,1,0:T(8,128)S(1)} %get-tuple-element.8, f32[66,34,130]{2,1,0:T(8,128)S(1)} %get-tuple-element.9), kind=kLoop, calls=%fused_computation.46 | loop fusion | flops 9961472 | bytes 19922944 | tf_op jit(solution)/shard_map/add | solution.py:39
  79.2 3.6 %collective-permute-start.6 = (f32[1,32,128]{2,1,0:T(8,128)S(1)}, f32[1,32,128]{2,1,0:T(8,128)S(1)}, u32[]{:S(2)}, u32[]{:S(2)}) collective-permute-start(f32[1,32,128]{2,1,0:T(8,128)S(1)} %get-tuple-element.20), channel_id=1, source_target_pairs={{16,0},{32,16},{48,32},{64,48},{80,64},{96,80},{112,96},{128,112},... | collective-permute-start | bytes 49160 | tf_op jit(solution)/shard_map/ppermute | solution.py:17
  88.1 3.4 %collective-permute-start.9 = (f32[66,32,1]{0,1,2:T(8,128)S(1)}, f32[66,32,1]{0,1,2:T(8,128)S(1)}, u32[]{:S(2)}, u32[]{:S(2)}) collective-permute-start(f32[66,32,1]{0,1,2:T(8,128)S(1)} %copy.33), channel_id=1, source_target_pairs={{0,4},{4,8},{8,12},{1,5},{5,9},{9,13},{2,6},{6,10},{10,14},{3,7},{... | collective-permute-start | bytes 25352 | tf_op jit(solution)/shard_map/ppermute | solution.py:14
  94.7 2.0 copy.34
  96.7 2.8 collective-permute-done.8
  101.5 2.0 pad_maximum_fusion.23
  103.5 3.4 %collective-permute-start.11 = (f32[66,1,130]{2,1,0:T(1,128)S(1)}, f32[66,1,130]{2,1,0:T(1,128)S(1)}, u32[]{:S(2)}, u32[]{:S(2)}) collective-permute-start(f32[66,1,130]{2,1,0:T(1,128)S(1)} %get-tuple-element.11), channel_id=1, source_target_pairs={{0,1},{1,2},{2,3},{4,5},{5,6},{6,7},{8,9},{9,10},{10,11},{12,13},{... | collective-permute-start | bytes 102968 | tf_op jit(solution)/shard_map/ppermute | solution.py:14
  108.9 5.0 %collective-permute-done.10 = f32[66,1,130]{2,1,0:T(1,128)S(1)} collective-permute-done((f32[66,1,130]{2,1,0:T(1,128)S(1)}, f32[66,1,130]{2,1,0:T(1,128)S(1)}, u32[]{:S(2)}, u32[]{:S(2)}) %collective-permute-start.10) | collective-permute-done | bytes 34352 | tf_op jit(solution)/shard_map/ppermute | solution.py:17
  113.9 12.4 %add_bitcast_fusion.1 = f32[1,64,32,128]{3,2,1,0:T(8,128)} fusion(f32[66,34,130]{2,1,0:T(8,128)S(1)} %get-tuple-element.8, f32[66,34,130]{2,1,0:T(8,128)} %copy-done.2, f32[66,34,130]{2,1,0:T(8,128)S(1)} %copy-done.1, f32[64,32,128]{2,1,0:T(8,128)} %copy-done.6, f32[1,32,128]{2,1,0:T(8,128)S(1)} %collective-permute-done.6, ...), kind=kLoop, calls=%fused_computation.44 | loop fusion | flops 15990784 | bytes 11652640 | tf_op jit(solution)/shard_map/stack | solution.py:57
  126.4 7.1 %add_bitcast_fusion = f32[1,64,32,128]{3,2,1,0:T(8,128)} fusion(f32[66,34,130]{2,1,0:T(8,128)S(1)} %copy-done.1, f32[66,34,130]{2,1,0:T(8,128)S(1)} %copy-done.3, f32[66,34,130]{2,1,0:T(8,128)S(1)} %get-tuple-element.8, f32[64,32,128]{2,1,0:T(8,128)S(1)} %copy-done.7, f32[1,32,128]{2,1,0:T(8,128)S(1)} %collective-permute-done.6, ...), kind=kLoop, calls=%fused_computation.43 | loop fusion | flops 15990784 | bytes 11652640 | tf_op jit(solution)/shard_map/stack | solution.py:57
  133.5 7.0 %add_bitcast_fusion.2 = f32[1,64,32,128]{3,2,1,0:T(8,128)} fusion(f32[66,34,130]{2,1,0:T(8,128)S(1)} %copy-done.3, f32[66,34,130]{2,1,0:T(8,128)S(1)} %get-tuple-element.8, f32[66,34,130]{2,1,0:T(8,128)S(1)} %copy-done.1, f32[64,32,128]{2,1,0:T(8,128)S(1)} %copy-done.7, f32[1,32,128]{2,1,0:T(8,128)S(1)} %collective-permute-done.6, ...), kind=kLoop, calls=%fused_computation.45 | loop fusion | flops 15990784 | bytes 11652640 | tf_op jit(solution)/shard_map/stack | solution.py:57
  140.5 108.2 %all-gather.3.cloned.1.call-done = f32[16384,1152]{1,0:T(8,128)} async-done(((f32[64,1152]{1,0:T(8,128)}), f32[16384,1152]{1,0:T(8,128)}) %all-gather.3.cloned.1.call-update) | async-done | bytes 75497488 | tf_op jit(solution)/shard_map/all_gather | solution.py:96
  248.8 23.7 %reduce_sum.18 = f32[64,1152]{1,0:T(8,128)S(1)} reduce(f32[256,64,1152]{2,1,0:T(8,128)} %bitcast.10, f32[]{:T(128)} %constant.20.clone.1), dimensions={0}, to_apply=%region_0.0 | reduce | flops 18800640 | bytes 75792384 | tf_op jit(solution)/shard_map/reduce_sum | solution.py:96
  273.4 3.7 %fusion = f32[2,3,4096]{2,1,0:T(4,128)S(1)} fusion(bf16[2,3,384]{2,1,0:T(4,128)(2,1)S(1)} %reshape.31, bf16[1,1,1,2,384,4096]{5,4,3,2,1,0:T(8,128)(2,1)} %param.8), kind=kOutput, calls=%fused_computation.1 | convolution fusion | flops 18874368 | bytes 6394368 | tf_op jit(solution)/shard_map/axz,ahx->ahz/dot_general | solution.py:99
  280.5 2.4 bitcast_add_fusion
  (76 shorter events, 25.8 us)
Async XLA Ops:
  7.2 4.7 %copy-start.18 = (s32[1,1,1,2]{3,2,1,0:T(1,128)S(1)}, s32[1,1,1,2]{3,2,1,0:T(1,128)}, u32[]{:S(2)}) copy-start(s32[1,1,1,2]{3,2,1,0:T(1,128)} %param.7) | copy-start | bytes 28
  7.2 241.6 %all-gather.3.cloned.1.call-start = ((), (), s32[]{:S(2)}) async-start(), calls=%async_computation | async-start | bytes 75792384 | tf_op jit(solution)/shard_map/all_gather | solution.py:96
  14.8 4.5 %copy-start.17 = (s32[1,1,1,2]{3,2,1,0:T(1,128)S(1)}, s32[1,1,1,2]{3,2,1,0:T(1,128)}, u32[]{:S(2)}) copy-start(s32[1,1,1,2]{3,2,1,0:T(1,128)} %param.6) | copy-start | bytes 28
  21.4 5.6 %collective-permute-start = (f32[3,1,32,128]{3,2,1,0:T(8,128)S(1)}, f32[3,1,32,128]{3,2,1,0:T(8,128)S(1)}, u32[]{:S(2)}, u32[]{:S(2)}) collective-permute-start(f32[3,1,32,128]{3,2,1,0:T(8,128)S(1)} %get-tuple-element.16), channel_id=1, source_target_pairs={{0,16},{16,32},{32,48},{48,64},{64,80},{80,96},{96,112},{112,128},... | collective-permute-start | bytes 147464 | tf_op jit(solution)/shard_map/ppermute | solution.py:14
  23.3 5.9 %collective-permute-start.1 = (f32[3,1,32,128]{3,2,1,0:T(8,128)S(1)}, f32[3,1,32,128]{3,2,1,0:T(8,128)S(1)}, u32[]{:S(2)}, u32[]{:S(2)}) collective-permute-start(f32[3,1,32,128]{3,2,1,0:T(8,128)S(1)} %get-tuple-element.15), channel_id=1, source_target_pairs={{16,0},{32,16},{48,32},{64,48},{80,64},{96,80},{112,96},{128,112},... | collective-permute-start | bytes 147464 | tf_op jit(solution)/shard_map/ppermute | solution.py:17
  29.2 3.9 %copy-start.4 = (f32[3,66,32,128]{3,2,1,0:T(8,128)}, f32[3,66,32,128]{3,2,1,0:T(8,128)S(1)}, u32[]{:S(2)}) copy-start(f32[3,66,32,128]{3,2,1,0:T(8,128)S(1)} %constant_dynamic-update-slice_fusion) | copy-start | bytes 9732100
  35.9 7.5 %collective-permute-start.2 = (f32[3,66,32,1]{1,2,3,0:T(8,128)S(1)}, f32[3,66,32,1]{1,2,3,0:T(8,128)S(1)}, u32[]{:S(2)}, u32[]{:S(2)}) collective-permute-start(f32[3,66,32,1]{1,2,3,0:T(8,128)S(1)} %copy.27), channel_id=1, source_target_pairs={{0,4},{4,8},{8,12},{1,5},{5,9},{9,13},{2,6},{6,10},{10,14},{3,7},{... | collective-permute-start | bytes 76040 | tf_op jit(solution)/shard_map/ppermute | solution.py:14
  42.1 6.2 %collective-permute-start.3 = (f32[3,66,32,1]{1,2,3,0:T(8,128)S(1)}, f32[3,66,32,1]{1,2,3,0:T(8,128)S(1)}, u32[]{:S(2)}, u32[]{:S(2)}) collective-permute-start(f32[3,66,32,1]{1,2,3,0:T(8,128)S(1)} %copy.28), channel_id=1, source_target_pairs={{4,0},{8,4},{12,8},{5,1},{9,5},{13,9},{6,2},{10,6},{14,10},{7,3},{... | collective-permute-start | bytes 76040 | tf_op jit(solution)/shard_map/ppermute | solution.py:17
  50.9 16.9 %copy-start.5 = (f32[3,66,32,128]{3,2,1,0:T(8,128)S(1)}, f32[3,66,32,128]{3,2,1,0:T(8,128)}, u32[]{:S(2)}) copy-start(f32[3,66,32,128]{3,2,1,0:T(8,128)} %copy-done.4) | copy-start | bytes 9732100
  50.9 16.9 %copy-start.8 = (f32[3,66,32,1]{3,2,1,0:T(8,128)S(1)}, f32[3,66,32,1]{3,2,1,0:T(8,128)}, u32[]{:S(2)}) copy-start(f32[3,66,32,1]{3,2,1,0:T(8,128)} %copy.29) | copy-start | bytes 76036
  50.9 16.9 %copy-start.9 = (f32[3,66,32,1]{3,2,1,0:T(8,128)S(1)}, f32[3,66,32,1]{3,2,1,0:T(8,128)}, u32[]{:S(2)}) copy-start(f32[3,66,32,1]{3,2,1,0:T(8,128)} %copy.30) | copy-start | bytes 76036
  54.8 8.9 %collective-permute-start.4 = (f32[3,66,1,130]{3,2,1,0:T(1,128)S(1)}, f32[3,66,1,130]{3,2,1,0:T(1,128)S(1)}, u32[]{:S(2)}, u32[]{:S(2)}) collective-permute-start(f32[3,66,1,130]{3,2,1,0:T(1,128)S(1)} %get-tuple-element.6), channel_id=1, source_target_pairs={{0,1},{1,2},{2,3},{4,5},{5,6},{6,7},{8,9},{9,10},{10,11},{12,13},{... | collective-permute-start | bytes 308888 | tf_op jit(solution)/shard_map/ppermute | solution.py:14
  58.6 9.3 %collective-permute-start.5 = (f32[3,66,1,130]{3,2,1,0:T(1,128)S(1)}, f32[3,66,1,130]{3,2,1,0:T(1,128)S(1)}, u32[]{:S(2)}, u32[]{:S(2)}) collective-permute-start(f32[3,66,1,130]{3,2,1,0:T(1,128)S(1)} %get-tuple-element.7), channel_id=1, source_target_pairs={{1,0},{2,1},{3,2},{5,4},{6,5},{7,6},{9,8},{10,9},{11,10},{13,12},{... | collective-permute-start | bytes 308888 | tf_op jit(solution)/shard_map/ppermute | solution.py:17
  72.4 4.8 %copy-start = (f32[66,34,130]{2,1,0:T(8,128)}, f32[66,34,130]{2,1,0:T(8,128)S(1)}, u32[]{:S(2)}) copy-start(f32[66,34,130]{2,1,0:T(8,128)S(1)} %get-tuple-element.9) | copy-start | bytes 3500644
  72.4 4.8 %copy-start.2 = (f32[66,34,130]{2,1,0:T(8,128)}, f32[66,34,130]{2,1,0:T(8,128)S(1)}, u32[]{:S(2)}) copy-start(f32[66,34,130]{2,1,0:T(8,128)S(1)} %get-tuple-element.10) | copy-start | bytes 3500644
  77.2 9.0 %copy-start.6 = (f32[64,32,128]{2,1,0:T(8,128)}, f32[64,32,128]{2,1,0:T(8,128)S(1)}, u32[]{:S(2)}) copy-start(f32[64,32,128]{2,1,0:T(8,128)S(1)} %sqrt_add_fusion) | copy-start | bytes 3145732
  77.3 5.6 %collective-permute-start.7 = (f32[1,32,128]{2,1,0:T(8,128)S(1)}, f32[1,32,128]{2,1,0:T(8,128)S(1)}, u32[]{:S(2)}, u32[]{:S(2)}) collective-permute-start(f32[1,32,128]{2,1,0:T(8,128)S(1)} %get-tuple-element.19), channel_id=1, source_target_pairs={{0,16},{16,32},{32,48},{48,64},{64,80},{80,96},{96,112},{112,128},... | collective-permute-start | bytes 49160 | tf_op jit(solution)/shard_map/ppermute | solution.py:14
  79.2 5.1 %collective-permute-start.6 = (f32[1,32,128]{2,1,0:T(8,128)S(1)}, f32[1,32,128]{2,1,0:T(8,128)S(1)}, u32[]{:S(2)}, u32[]{:S(2)}) collective-permute-start(f32[1,32,128]{2,1,0:T(8,128)S(1)} %get-tuple-element.20), channel_id=1, source_target_pairs={{16,0},{32,16},{48,32},{64,48},{80,64},{96,80},{112,96},{128,112},... | collective-permute-start | bytes 49160 | tf_op jit(solution)/shard_map/ppermute | solution.py:17
  88.1 6.6 %collective-permute-start.9 = (f32[66,32,1]{0,1,2:T(8,128)S(1)}, f32[66,32,1]{0,1,2:T(8,128)S(1)}, u32[]{:S(2)}, u32[]{:S(2)}) collective-permute-start(f32[66,32,1]{0,1,2:T(8,128)S(1)} %copy.33), channel_id=1, source_target_pairs={{0,4},{4,8},{8,12},{1,5},{5,9},{9,13},{2,6},{6,10},{10,14},{3,7},{... | collective-permute-start | bytes 25352 | tf_op jit(solution)/shard_map/ppermute | solution.py:14
  93.4 6.1 %collective-permute-start.8 = (f32[66,32,1]{0,1,2:T(8,128)S(1)}, f32[66,32,1]{0,1,2:T(8,128)S(1)}, u32[]{:S(2)}, u32[]{:S(2)}) collective-permute-start(f32[66,32,1]{0,1,2:T(8,128)S(1)} %copy.31), channel_id=1, source_target_pairs={{4,0},{8,4},{12,8},{5,1},{9,5},{13,9},{6,2},{10,6},{14,10},{7,3},{... | collective-permute-start | bytes 25352 | tf_op jit(solution)/shard_map/ppermute | solution.py:17
  101.5 12.4 %copy-start.1 = (f32[66,34,130]{2,1,0:T(8,128)S(1)}, f32[66,34,130]{2,1,0:T(8,128)}, u32[]{:S(2)}) copy-start(f32[66,34,130]{2,1,0:T(8,128)} %copy-done) | copy-start | bytes 3500644
  103.5 5.4 %collective-permute-start.11 = (f32[66,1,130]{2,1,0:T(1,128)S(1)}, f32[66,1,130]{2,1,0:T(1,128)S(1)}, u32[]{:S(2)}, u32[]{:S(2)}) collective-permute-start(f32[66,1,130]{2,1,0:T(1,128)S(1)} %get-tuple-element.11), channel_id=1, source_target_pairs={{0,1},{1,2},{2,3},{4,5},{5,6},{6,7},{8,9},{9,10},{10,11},{12,13},{... | collective-permute-start | bytes 102968 | tf_op jit(solution)/shard_map/ppermute | solution.py:14
  106.9 19.4 %copy-start.3 = (f32[66,34,130]{2,1,0:T(8,128)S(1)}, f32[66,34,130]{2,1,0:T(8,128)}, u32[]{:S(2)}) copy-start(f32[66,34,130]{2,1,0:T(8,128)} %copy-done.2) | copy-start | bytes 3500644
  106.9 19.4 %copy-start.7 = (f32[64,32,128]{2,1,0:T(8,128)S(1)}, f32[64,32,128]{2,1,0:T(8,128)}, u32[]{:S(2)}) copy-start(f32[64,32,128]{2,1,0:T(8,128)} %copy-done.6) | copy-start | bytes 3145732
  107.0 19.4 %copy-start.10 = (f32[66,32,1]{2,1,0:T(8,128)S(1)}, f32[66,32,1]{2,1,0:T(8,128)}, u32[]{:S(2)}) copy-start(f32[66,32,1]{2,1,0:T(8,128)} %copy.34) | copy-start | bytes 25348
  107.0 19.4 %copy-start.11 = (f32[66,32,1]{2,1,0:T(8,128)S(1)}, f32[66,32,1]{2,1,0:T(8,128)}, u32[]{:S(2)}) copy-start(f32[66,32,1]{2,1,0:T(8,128)} %copy.32) | copy-start | bytes 25348
  107.0 6.9 %collective-permute-start.10 = (f32[66,1,130]{2,1,0:T(1,128)S(1)}, f32[66,1,130]{2,1,0:T(1,128)S(1)}, u32[]{:S(2)}, u32[]{:S(2)}) collective-permute-start(f32[66,1,130]{2,1,0:T(1,128)S(1)} %get-tuple-element.12), channel_id=1, source_target_pairs={{1,0},{2,1},{3,2},{5,4},{6,5},{7,6},{9,8},{10,9},{11,10},{13,12},{... | collective-permute-start | bytes 102968 | tf_op jit(solution)/shard_map/ppermute | solution.py:17
  248.8 24.2 %copy-start.16 = (f32[64,384]{1,0:T(8,128)S(1)}, f32[64,384]{1,0:T(8,128)}, u32[]{:S(2)}) copy-start(f32[64,384]{1,0:T(8,128)} %param.9) | copy-start | bytes 294916
  273.2 4.0 %copy-start.15 = (f32[64,1152]{1,0:T(8,128)}, f32[64,1152]{1,0:T(8,128)S(1)}, u32[]{:S(2)}) copy-start(f32[64,1152]{1,0:T(8,128)S(1)} %mul.301) | copy-start | bytes 884740
  278.7 1.2 copy-start.12
  278.7 1.5 copy-start.13
  278.7 1.8 copy-start.14
Sparse Core Ops, SparseCore 0:
  20.6 228.1 all-gather.2
